TPU v7x, 32 devices: a whole 2x2x4 slice. The times are simulated.
32 devices in a mesh: groups: 2 (over x), ctx: 16 (over z, y, core).
Axes of the slice: x: 2, y: 2, z: 4, core: 2. Of those that a mesh axis runs over, the one named last changes fastest.
Arguments:
- queries: bfloat16 [3072, 16, 128], P(('groups', 'ctx')), parts along dimension 0, may hold values from -12 to 12
- keys: bfloat16 [3072, 4, 128], P(('groups', 'ctx')), parts along dimension 0, may hold values from -5 to 5
- values: bfloat16 [3072, 4, 128], P(('groups', 'ctx')), parts along dimension 0, may hold values from -6 to 6
- positions: int32 [3072], P(('groups', 'ctx')), parts along dimension 0, may hold values from 0 to 1535, as said below
Outputs:
- attended: bfloat16 [3072, 16, 128], P(('groups', 'ctx')), parts along dimension 0
There are 2 independent parts, one for each index of `groups`. A program takes and returns all parts, laid end to end along the dimension named above; each array names one. Nothing has to cross between parts.
Inputs may be any that keep to these rules, and one draw needn't show every extreme that they name: A permutation of 0 to 1535 in which the 96 rows of each device along ctx hold the positions c, c + 16, c + 32 and so on in that order, for one offset c a device, the offsets of the devices being a permutation of 0 to 15.
All inputs are finite; a program needn't handle non-finite values.
Results may differ from a plain program's by a relative error of at most 0.0091.
Values may be sent and summed in bfloat16 or wider, within the bound.
A program may use at most 64 MiB of HBM per device.

v0:
```python
import math

import jax
import jax.numpy as jnp
from jax import lax
from jax.sharding import PartitionSpec as P


def shortened(shard):

    def short(part):
        return part.astype(jnp.bfloat16) if part.dtype == jnp.float32 else part

    return jax.tree.map(short, shard)


def partner(block, axis, bit):
    count = lax.axis_size(axis)
    route = []
    for low in range(count):
        high = low | 1 << bit
        if high != low and high < count:
            route += [(low, high), (high, low)]
    return lax.ppermute(block, axis, route)


def from_behind(block, axis, distance):
    devices = range(lax.axis_size(axis))
    route = [((i - distance) % len(devices), i) for i in devices]
    return lax.ppermute(block, axis, route)


def rotate(tensor, places):
    half_size = tensor.shape[-1] // 2
    inverse = jnp.power(
        jnp.float32(1000000.0), -jnp.arange(half_size, dtype=jnp.float32) * 2.0 / tensor.shape[-1]
    )
    angles = places.astype(jnp.float32)[:, None] * inverse[None, :]
    cosine = jnp.cos(angles)[:, None, :]
    sines = jnp.sin(angles)[:, None, :]
    floats = tensor.astype(jnp.float32)
    leading = floats[..., :half_size]
    trailing = floats[..., half_size:]
    return jnp.concatenate(
        [leading * cosine - trailing * sines, trailing * cosine + leading * sines], -1
    ).astype(jnp.bfloat16)


def attend_block(carried, grouped, query_places, key_block, value_block, key_places, scaling):
    maxima, totals, weighted = carried
    scores = (
        jnp.einsum("tkgd,skd->kgts", grouped, key_block, preferred_element_type=jnp.float32)
        * scaling
    )
    allowed = query_places[:, None] >= key_places[None, :]
    scores = jnp.where(allowed[None, None], scores, -jnp.inf)
    new_max = jnp.maximum(maxima, jnp.max(scores, axis=-1))
    safe_max = jnp.where(new_max == -jnp.inf, 0.0, new_max)
    weights = jnp.exp(scores - safe_max[..., None])
    shrink = jnp.exp(maxima - safe_max)
    totals = totals * shrink + jnp.sum(weights, axis=-1)
    rounded = weights.astype(jnp.bfloat16)
    weighted = weighted * shrink[..., None] + jnp.einsum(
        "kgts,skd->kgtd", rounded, value_block, preferred_element_type=jnp.float32
    )
    return (new_max, totals, weighted)


def butterfly(members, device_index, group_size, backward):
    levels = group_size.bit_length() - 1
    for level_index in range(levels):
        span_size = 1 << level_index
        own_bit = device_index // span_size % 2
        halves = []
        outgoing = []
        for member in members:
            shaped = member.reshape(
                (group_size // (2 * span_size), 2, span_size) + member.shape[1:]
            )
            lower_half = shaped[:, 0]
            upper_half = shaped[:, 1]
            halves.append((lower_half, upper_half))
            outgoing.append(jnp.where(own_bit == 0, upper_half, lower_half))
        if backward:
            received = partner(shortened(tuple(outgoing)), "ctx", level_index)
        else:
            received = partner(shortened(tuple(outgoing)), "ctx", level_index)
        updated = []
        for position_index in range(len(members)):
            lower_half, upper_half = halves[position_index]
            incoming = received[position_index]
            new_lower = jnp.where(own_bit == 0, lower_half, incoming)
            new_upper = jnp.where(own_bit == 0, incoming, upper_half)
            joined = jnp.stack([new_lower, new_upper], axis=1)
            updated.append(joined.reshape(members[position_index].shape))
        members = tuple(updated)
    return members


def shards(queries, keys, values, positions):
    tokens, head_count, head_size = queries.shape
    kv_heads = keys.shape[1]
    per_group = head_count // kv_heads
    scaling = 1.0 / math.sqrt(head_size)
    q_rot = rotate(queries, positions)
    k_rot = rotate(keys, positions)
    grouped = q_rot.reshape(tokens, kv_heads, per_group, head_size)
    device_index = lax.axis_index("ctx")
    places_copy = jnp.broadcast_to(positions[None, :], (kv_heads, tokens))
    query_slots = grouped.transpose(1, 0, 2, 3)
    key_slots = k_rot.transpose(1, 0, 2)
    value_slots = values.transpose(1, 0, 2)
    query_slots, key_slots, value_slots, places_copy = butterfly(
        (query_slots, key_slots, value_slots, places_copy), device_index, kv_heads, False
    )
    group_rows = kv_heads * tokens
    local_query = query_slots.reshape(group_rows, 1, per_group, head_size)
    local_keys = key_slots.reshape(group_rows, 1, head_size)
    local_values = value_slots.reshape(group_rows, 1, head_size)
    local_places = places_copy.reshape(group_rows)
    starting = (
        jnp.full((1, per_group, group_rows), -jnp.inf, jnp.float32),
        jnp.zeros((1, per_group, group_rows), jnp.float32),
        jnp.zeros((1, per_group, group_rows, head_size), jnp.float32),
    )
    running = attend_block(
        starting, local_query, local_places, local_keys, local_values, local_places, scaling
    )

    def advance_cycle(state, unused):
        moving, partial_value = state
        moving = from_behind((moving[0], moving[1], shortened(moving[2])), "ctx", kv_heads)
        partial_value = attend_block(
            partial_value, local_query, local_places, moving[0], moving[1], moving[2], scaling
        )
        return ((moving, partial_value), None)

    final_state, unused = lax.scan(
        advance_cycle,
        ((local_keys, local_values, local_places), running),
        None,
        length=lax.axis_size("ctx") // kv_heads - 1,
    )
    maxima, totals, weighted = final_state[1]
    result = (weighted / totals[..., None]).astype(jnp.bfloat16)
    slots = result.reshape(per_group, kv_heads, tokens, head_size).transpose(1, 2, 0, 3)
    returned = butterfly((slots,), device_index, kv_heads, True)[0]
    return returned.transpose(1, 0, 2, 3).reshape(tokens, head_count, head_size)


def solution(mesh):
    placed = (
        P(("groups", "ctx"), None, None),
        P(("groups", "ctx"), None, None),
        P(("groups", "ctx"), None, None),
        P(("groups", "ctx")),
    )
    return jax.shard_map(
        shards,
        mesh=mesh,
        in_specs=placed,
        out_specs=P(("groups", "ctx"), None, None),
        check_vma=False,
    )
```

profile of v0, /device:TPU:0, one launch (start us, length us, event | category | flops | bytes accessed | tf_op | source)
XLA Modules:
  0.0 63.8 jit_solution(14075965202426337271)
XLA Ops:
  0.7 1.0 %convert_element_type.24 = f32[96,16,128]{2,1,0:T(8,128)S(1)} convert(bf16[96,16,128]{2,1,0:T(8,128)(2,1)} %param.6) | non-fusion elementwise | flops 196608 | bytes 1179648 | tf_op jit(solution)/shard_map/convert_element_type | solution.py:41
  5.5 2.9 %collective-permute-start.8 = (s32[1,2,96]{2,1,0:T(2,128)S(1)}, s32[1,2,96]{2,1,0:T(2,128)S(1)}, u32[]{:S(2)}, u32[]{:S(2)}) collective-permute-start(s32[1,2,96]{2,1,0:T(2,128)S(1)} %broadcast_select_fusion.10), channel_id=1, source_target_pairs={{0,2},{2,0},{1,3},{3,1},{4,6},{6,4},{5,7},{7,5},{8,10},{10,8},{9,1... | collective-permute-start | bytes 2312 | tf_op jit(solution)/shard_map/ppermute | solution.py:24
  8.5 1.5 %collective-permute-done.8 = s32[1,2,96]{2,1,0:T(2,128)S(1)} collective-permute-done((s32[1,2,96]{2,1,0:T(2,128)S(1)}, s32[1,2,96]{2,1,0:T(2,128)S(1)}, u32[]{:S(2)}, u32[]{:S(2)}) %collective-permute-start.8) | collective-permute-done | bytes 800 | tf_op jit(solution)/shard_map/ppermute | solution.py:24
  10.3 2.1 %collective-permute-start.4 = (bf16[1,2,96,128]{3,2,1,0:T(8,128)(2,1)S(1)}, bf16[1,2,96,128]{3,2,1,0:T(8,128)(2,1)S(1)}, u32[]{:S(2)}, u32[]{:S(2)}) collective-permute-start(bf16[1,2,96,128]{3,2,1,0:T(8,128)(2,1)S(1)} %broadcast_select_fusion.7), channel_id=1, source_target_pairs={{0,2},{2,0},{1,3},{3,1},{4,6},{6,4},{5,7},{7,5},{8,10},{10,8},{9,1... | collective-permute-start | bytes 147464 | tf_op jit(solution)/shard_map/ppermute | solution.py:24
  12.6 2.4 %collective-permute-done.4 = bf16[1,2,96,128]{3,2,1,0:T(8,128)(2,1)S(1)} collective-permute-done((bf16[1,2,96,128]{3,2,1,0:T(8,128)(2,1)S(1)}, bf16[1,2,96,128]{3,2,1,0:T(8,128)(2,1)S(1)}, u32[]{:S(2)}, u32[]{:S(2)}) %collective-permute-start.4) | collective-permute-done | bytes 49184 | tf_op jit(solution)/shard_map/ppermute | solution.py:24
  15.0 1.7 %collective-permute-done.6 = bf16[1,2,96,128]{3,2,1,0:T(8,128)(2,1)S(1)} collective-permute-done((bf16[1,2,96,128]{3,2,1,0:T(8,128)(2,1)S(1)}, bf16[1,2,96,128]{3,2,1,0:T(8,128)(2,1)S(1)}, u32[]{:S(2)}, u32[]{:S(2)}) %collective-permute-start.6) | collective-permute-done | bytes 49184 | tf_op jit(solution)/shard_map/ppermute | solution.py:24
  17.3 5.2 %collective-permute-done.10 = bf16[1,2,96,4,128]{4,2,3,1,0:T(8,128)(2,1)S(1)} collective-permute-done((bf16[1,2,96,4,128]{4,2,3,1,0:T(8,128)(2,1)S(1)}, bf16[1,2,96,4,128]{4,2,3,1,0:T(8,128)(2,1)S(1)}, u32[]{:S(2)}, u32[]{:S(2)}) %collective-permute-start.10) | collective-permute-done | bytes 196640 | tf_op jit(solution)/shard_map/ppermute | solution.py:24
  24.6 29.2 %while.21 = (s32[]{:T(128)}, bf16[384,1,128]{2,0,1:T(8,128)(2,1)S(1)}, bf16[384,1,128]{2,0,1:T(8,128)(2,1)S(1)}, s32[384]{0:T(512)S(1)}, f32[1,4,384]{2,1,0:T(4,...) while((s32[]{:T(128)}, ...), condition=%wide.wide.region_5.6_spmd, body=%wide.wide.region_2.5_spmd.sunk | while | flops 309032448 | bytes 11133157 | solution.py:138
  24.6 1.6 %collective-permute-start.2 = (s32[384]{0:T(512)S(1)}, s32[384]{0:T(512)S(1)}, u32[]{:S(2)}, u32[]{:S(2)}) collective-permute-start(s32[384]{0:T(512)S(1)} %get-tuple-element.234), channel_id=1, source_target_pairs={{12,0},{13,1},{14,2},{15,3},{0,4},{1,5},{2,6},{3,7},{4,8},{5,9},{6... | collective-permute-start | bytes 4616 | tf_op jit(solution)/shard_map/while/body/eval_jaxpr/ppermute | solution.py:30
  26.2 1.6 %collective-permute-start = (bf16[384,1,128]{2,0,1:T(8,128)(2,1)S(1)}, bf16[384,1,128]{2,0,1:T(8,128)(2,1)S(1)}, u32[]{:S(2)}, u32[]{:S(2)}) collective-permute-start(bf16[384,1,128]{2,0,1:T(8,128)(2,1)S(1)} %get-tuple-element.232), channel_id=1, source_target_pairs={{12,0},{13,1},{14,2},{15,3},{0,4},{1,5},{2,6},{3,7},{4,8},{5,9},{6... | collective-permute-start | bytes 294920 | tf_op jit(solution)/shard_map/while/body/eval_jaxpr/ppermute | solution.py:30
  27.8 1.6 %collective-permute-start.1 = (bf16[384,1,128]{2,0,1:T(8,128)(2,1)S(1)}, bf16[384,1,128]{2,0,1:T(8,128)(2,1)S(1)}, u32[]{:S(2)}, u32[]{:S(2)}) collective-permute-start(bf16[384,1,128]{2,0,1:T(8,128)(2,1)S(1)} %get-tuple-element.233), channel_id=1, source_target_pairs={{12,0},{13,1},{14,2},{15,3},{0,4},{1,5},{2,6},{3,7},{4,8},{5,9},{6... | collective-permute-start | bytes 294920 | tf_op jit(solution)/shard_map/while/body/eval_jaxpr/ppermute | solution.py:30
  30.2 2.4 %collective-permute-done = bf16[384,1,128]{2,0,1:T(8,128)(2,1)S(1)} collective-permute-done((bf16[384,1,128]{2,0,1:T(8,128)(2,1)S(1)}, bf16[384,1,128]{2,0,1:T(8,128)(2,1)S(1)}, u32[]{:S(2)}, u32[]{:S(2)}) %collective-permute-start) | collective-permute-done | bytes 98336 | tf_op jit(solution)/shard_map/while/body/eval_jaxpr/ppermute | solution.py:30
  34.2 0.9 %fusion.59 = f32[1,4,384,128]{3,2,1,0:T(8,128)S(1)} fusion(f32[384,384,4]{1,0,2:T(8,128)S(1)} %get-tuple-element.218, f32[4,384]{1,0:T(4,128)S(1)} %fusion.57, pred[384,384]{0,1:T(8,128)(4,1)S(1)} %broadcast_compare_fusion.4, f32[1,4,384,128]{3,2,1,0:T(8,128)S(1)} %get-tuple-element.237, f32[4,384]{1,0:T(4,128)S(1)} %get-tuple-element.219, ...), kind=kOutput, calls=%fused_computation.6.clone.clone.1 | convolution fusion | flops 153747456 | bytes 4190208 | tf_op jit(solution)/shard_map/while/body/eval_jaxpr/kgts,skd->kgtd/dot_general | solution.py:63
  35.5 1.2 %collective-permute-start = (bf16[384,1,128]{2,0,1:T(8,128)(2,1)S(1)}, bf16[384,1,128]{2,0,1:T(8,128)(2,1)S(1)}, u32[]{:S(2)}, u32[]{:S(2)}) collective-permute-start(bf16[384,1,128]{2,0,1:T(8,128)(2,1)S(1)} %get-tuple-element.232), channel_id=1, source_target_pairs={{12,0},{13,1},{14,2},{15,3},{0,4},{1,5},{2,6},{3,7},{4,8},{5,9},{6... | collective-permute-start | bytes 294920 | tf_op jit(solution)/shard_map/while/body/eval_jaxpr/ppermute | solution.py:30
  36.8 3.8 %collective-permute-done.2 = s32[384]{0:T(512)S(1)} collective-permute-done((s32[384]{0:T(512)S(1)}, s32[384]{0:T(512)S(1)}, u32[]{:S(2)}, u32[]{:S(2)}) %collective-permute-start.2) | collective-permute-done | bytes 1568 | tf_op jit(solution)/shard_map/while/body/eval_jaxpr/ppermute | solution.py:30
  40.8 1.2 %collective-permute-done = bf16[384,1,128]{2,0,1:T(8,128)(2,1)S(1)} collective-permute-done((bf16[384,1,128]{2,0,1:T(8,128)(2,1)S(1)}, bf16[384,1,128]{2,0,1:T(8,128)(2,1)S(1)}, u32[]{:S(2)}, u32[]{:S(2)}) %collective-permute-start) | collective-permute-done | bytes 98336 | tf_op jit(solution)/shard_map/while/body/eval_jaxpr/ppermute | solution.py:30
  43.1 1.1 %collective-permute-done.1 = bf16[384,1,128]{2,0,1:T(8,128)(2,1)S(1)} collective-permute-done((bf16[384,1,128]{2,0,1:T(8,128)(2,1)S(1)}, bf16[384,1,128]{2,0,1:T(8,128)(2,1)S(1)}, u32[]{:S(2)}, u32[]{:S(2)}) %collective-permute-start.1) | collective-permute-done | bytes 98336 | tf_op jit(solution)/shard_map/while/body/eval_jaxpr/ppermute | solution.py:30
  44.2 0.9 %fusion.59 = f32[1,4,384,128]{3,2,1,0:T(8,128)S(1)} fusion(f32[384,384,4]{1,0,2:T(8,128)S(1)} %get-tuple-element.218, f32[4,384]{1,0:T(4,128)S(1)} %fusion.57, pred[384,384]{0,1:T(8,128)(4,1)S(1)} %broadcast_compare_fusion.4, f32[1,4,384,128]{3,2,1,0:T(8,128)S(1)} %get-tuple-element.237, f32[4,384]{1,0:T(4,128)S(1)} %get-tuple-element.219, ...), kind=kOutput, calls=%fused_computation.6.clone.clone.1 | convolution fusion | flops 153747456 | bytes 4190208 | tf_op jit(solution)/shard_map/while/body/eval_jaxpr/kgts,skd->kgtd/dot_general | solution.py:63
  45.2 1.0 %collective-permute-start = (bf16[384,1,128]{2,0,1:T(8,128)(2,1)S(1)}, bf16[384,1,128]{2,0,1:T(8,128)(2,1)S(1)}, u32[]{:S(2)}, u32[]{:S(2)}) collective-permute-start(bf16[384,1,128]{2,0,1:T(8,128)(2,1)S(1)} %get-tuple-element.232), channel_id=1, source_target_pairs={{12,0},{13,1},{14,2},{15,3},{0,4},{1,5},{2,6},{3,7},{4,8},{5,9},{6... | collective-permute-start | bytes 294920 | tf_op jit(solution)/shard_map/while/body/eval_jaxpr/ppermute | solution.py:30
  46.2 1.8 %collective-permute-start.1 = (bf16[384,1,128]{2,0,1:T(8,128)(2,1)S(1)}, bf16[384,1,128]{2,0,1:T(8,128)(2,1)S(1)}, u32[]{:S(2)}, u32[]{:S(2)}) collective-permute-start(bf16[384,1,128]{2,0,1:T(8,128)(2,1)S(1)} %get-tuple-element.233), channel_id=1, source_target_pairs={{12,0},{13,1},{14,2},{15,3},{0,4},{1,5},{2,6},{3,7},{4,8},{5,9},{6... | collective-permute-start | bytes 294920 | tf_op jit(solution)/shard_map/while/body/eval_jaxpr/ppermute | solution.py:30
  48.0 2.6 %collective-permute-done.2 = s32[384]{0:T(512)S(1)} collective-permute-done((s32[384]{0:T(512)S(1)}, s32[384]{0:T(512)S(1)}, u32[]{:S(2)}, u32[]{:S(2)}) %collective-permute-start.2) | collective-permute-done | bytes 1568 | tf_op jit(solution)/shard_map/while/body/eval_jaxpr/ppermute | solution.py:30
  54.2 1.4 %collective-permute-done.11 = bf16[2,1,96,4,128]{4,2,3,0,1:T(8,128)(2,1)S(1)} collective-permute-done((bf16[2,1,96,4,128]{4,2,3,0,1:T(8,128)(2,1)S(1)}, bf16[2,1,96,4,128]{4,2,3,0,1:T(8,128)(2,1)S(1)}, u32[]{:S(2)}, u32[]{:S(2)}) %collective-permute-start.11) | collective-permute-done | bytes 196640 | tf_op jit(solution)/shard_map/ppermute | solution.py:24
  56.6 6.2 %collective-permute-done.12 = bf16[1,2,96,4,128]{4,2,3,1,0:T(8,128)(2,1)S(1)} collective-permute-done((bf16[1,2,96,4,128]{4,2,3,1,0:T(8,128)(2,1)S(1)}, bf16[1,2,96,4,128]{4,2,3,1,0:T(8,128)(2,1)S(1)}, u32[]{:S(2)}, u32[]{:S(2)}) %collective-permute-start.12) | collective-permute-done | bytes 196640 | tf_op jit(solution)/shard_map/ppermute | solution.py:24
  62.9 0.9 %copy.58 = bf16[96,4,4,128]{3,2,1,0:T(4,128)(2,1)} copy(bf16[96,4,4,128]{3,0,2,1:T(8,128)(2,1)S(1)} %bitcast.310) | data formatting | bytes 786432 | tf_op jit(solution)/shard_map/transpose | solution.py:148
  (111 shorter events, 16.1 us)
Async XLA Ops:
  2.0 1.5 %copy-start.1 = (bf16[96,4,128]{2,1,0:T(4,128)(2,1)S(1)}, bf16[96,4,128]{2,1,0:T(4,128)(2,1)}, u32[]{:S(2)}) copy-start(bf16[96,4,128]{2,1,0:T(4,128)(2,1)} %param.7) | copy-start | bytes 294916
  2.5 1.6 %copy-start.3 = (s32[96]{0:T(128)S(1)}, s32[96]{0:T(128)}, u32[]{:S(2)}) copy-start(s32[96]{0:T(128)} %param.9) | copy-start | bytes 1156
  2.5 2.1 %copy-start = (bf16[96,4,128]{2,1,0:T(4,128)(2,1)S(1)}, bf16[96,4,128]{2,1,0:T(4,128)(2,1)}, u32[]{:S(2)}) copy-start(bf16[96,4,128]{2,1,0:T(4,128)(2,1)} %param.8) | copy-start | bytes 294916
  2.9 13.8 %collective-permute-start.9 = (bf16[2,1,96,4,128]{4,2,3,0,1:T(8,128)(2,1)S(1)}, bf16[2,1,96,4,128]{4,2,3,0,1:T(8,128)(2,1)S(1)}, u32[]{:S(2)}, u32[]{:S(2)}) collective-permute-start(bf16[2,1,96,4,128]{4,2,3,0,1:T(8,128)(2,1)S(1)} %broadcast_select_fusion.1), channel_id=1, source_target_pairs={{0,1},{1,0},{2,3},{3,2},{4,5},{5,4},{6,7},{7,6},{8,9},{9,8},{10,11... | collective-permute-start | bytes 589832 | tf_op jit(solution)/shard_map/ppermute | solution.py:24
  4.0 6.2 %collective-permute-start.3 = (bf16[2,1,96,128]{3,2,0,1:T(8,128)(2,1)S(1)}, bf16[2,1,96,128]{3,2,0,1:T(8,128)(2,1)S(1)}, u32[]{:S(2)}, u32[]{:S(2)}) collective-permute-start(bf16[2,1,96,128]{3,2,0,1:T(8,128)(2,1)S(1)} %broadcast_select_fusion.5), channel_id=1, source_target_pairs={{0,1},{1,0},{2,3},{3,2},{4,5},{5,4},{6,7},{7,6},{8,9},{9,8},{10,11... | collective-permute-start | bytes 147464 | tf_op jit(solution)/shard_map/ppermute | solution.py:24
  4.1 1.3 %collective-permute-start.7 = (s32[2,1,96]{2,0,1:T(2,128)S(1)}, s32[2,1,96]{2,0,1:T(2,128)S(1)}, u32[]{:S(2)}, u32[]{:S(2)}) collective-permute-start(s32[2,1,96]{2,0,1:T(2,128)S(1)} %squeeze.66), channel_id=1, source_target_pairs={{0,1},{1,0},{2,3},{3,2},{4,5},{5,4},{6,7},{7,6},{8,9},{9,8},{10,11... | collective-permute-start | bytes 2312 | tf_op jit(solution)/shard_map/ppermute | solution.py:24
  5.5 4.5 %collective-permute-start.8 = (s32[1,2,96]{2,1,0:T(2,128)S(1)}, s32[1,2,96]{2,1,0:T(2,128)S(1)}, u32[]{:S(2)}, u32[]{:S(2)}) collective-permute-start(s32[1,2,96]{2,1,0:T(2,128)S(1)} %broadcast_select_fusion.10), channel_id=1, source_target_pairs={{0,2},{2,0},{1,3},{3,1},{4,6},{6,4},{5,7},{7,5},{8,10},{10,8},{9,1... | collective-permute-start | bytes 2312 | tf_op jit(solution)/shard_map/ppermute | solution.py:24
  8.4 4.0 %collective-permute-start.5 = (bf16[2,1,96,128]{3,2,0,1:T(8,128)(2,1)S(1)}, bf16[2,1,96,128]{3,2,0,1:T(8,128)(2,1)S(1)}, u32[]{:S(2)}, u32[]{:S(2)}) collective-permute-start(bf16[2,1,96,128]{3,2,0,1:T(8,128)(2,1)S(1)} %broadcast_select_fusion.4), channel_id=1, source_target_pairs={{0,1},{1,0},{2,3},{3,2},{4,5},{5,4},{6,7},{7,6},{8,9},{9,8},{10,11... | collective-permute-start | bytes 147464 | tf_op jit(solution)/shard_map/ppermute | solution.py:24
  10.0 7.4 %copy-start.2 = (s32[1,2,2,96]{3,2,1,0:T(2,128)}, s32[1,2,2,96]{3,2,1,0:T(2,128)S(1)}, u32[]{:S(2)}) copy-start(s32[1,2,2,96]{3,2,1,0:T(2,128)S(1)} %pad_add_fusion) | copy-start | bytes 4612
  10.3 4.6 %collective-permute-start.4 = (bf16[1,2,96,128]{3,2,1,0:T(8,128)(2,1)S(1)}, bf16[1,2,96,128]{3,2,1,0:T(8,128)(2,1)S(1)}, u32[]{:S(2)}, u32[]{:S(2)}) collective-permute-start(bf16[1,2,96,128]{3,2,1,0:T(8,128)(2,1)S(1)} %broadcast_select_fusion.7), channel_id=1, source_target_pairs={{0,2},{2,0},{1,3},{3,1},{4,6},{6,4},{5,7},{7,5},{8,10},{10,8},{9,1... | collective-permute-start | bytes 147464 | tf_op jit(solution)/shard_map/ppermute | solution.py:24
  12.5 4.2 %collective-permute-start.6 = (bf16[1,2,96,128]{3,2,1,0:T(8,128)(2,1)S(1)}, bf16[1,2,96,128]{3,2,1,0:T(8,128)(2,1)S(1)}, u32[]{:S(2)}, u32[]{:S(2)}) collective-permute-start(bf16[1,2,96,128]{3,2,1,0:T(8,128)(2,1)S(1)} %broadcast_select_fusion.6), channel_id=1, source_target_pairs={{0,2},{2,0},{1,3},{3,1},{4,6},{6,4},{5,7},{7,5},{8,10},{10,8},{9,1... | collective-permute-start | bytes 147464 | tf_op jit(solution)/shard_map/ppermute | solution.py:24
  16.8 5.7 %collective-permute-start.10 = (bf16[1,2,96,4,128]{4,2,3,1,0:T(8,128)(2,1)S(1)}, bf16[1,2,96,4,128]{4,2,3,1,0:T(8,128)(2,1)S(1)}, u32[]{:S(2)}, u32[]{:S(2)}) collective-permute-start(bf16[1,2,96,4,128]{4,2,3,1,0:T(8,128)(2,1)S(1)} %broadcast_select_fusion.3), channel_id=1, source_target_pairs={{0,2},{2,0},{1,3},{3,1},{4,6},{6,4},{5,7},{7,5},{8,10},{10,8},{9,1... | collective-permute-start | bytes 589832 | tf_op jit(solution)/shard_map/ppermute | solution.py:24
  24.6 5.4 %collective-permute-start.2 = (s32[384]{0:T(512)S(1)}, s32[384]{0:T(512)S(1)}, u32[]{:S(2)}, u32[]{:S(2)}) collective-permute-start(s32[384]{0:T(512)S(1)} %get-tuple-element.234), channel_id=1, source_target_pairs={{12,0},{13,1},{14,2},{15,3},{0,4},{1,5},{2,6},{3,7},{4,8},{5,9},{6... | collective-permute-start | bytes 4616 | tf_op jit(solution)/shard_map/while/body/eval_jaxpr/ppermute | solution.py:30
  26.2 6.4 %collective-permute-start = (bf16[384,1,128]{2,0,1:T(8,128)(2,1)S(1)}, bf16[384,1,128]{2,0,1:T(8,128)(2,1)S(1)}, u32[]{:S(2)}, u32[]{:S(2)}) collective-permute-start(bf16[384,1,128]{2,0,1:T(8,128)(2,1)S(1)} %get-tuple-element.232), channel_id=1, source_target_pairs={{12,0},{13,1},{14,2},{15,3},{0,4},{1,5},{2,6},{3,7},{4,8},{5,9},{6... | collective-permute-start | bytes 294920 | tf_op jit(solution)/shard_map/while/body/eval_jaxpr/ppermute | solution.py:30
  27.8 6.4 %collective-permute-start.1 = (bf16[384,1,128]{2,0,1:T(8,128)(2,1)S(1)}, bf16[384,1,128]{2,0,1:T(8,128)(2,1)S(1)}, u32[]{:S(2)}, u32[]{:S(2)}) collective-permute-start(bf16[384,1,128]{2,0,1:T(8,128)(2,1)S(1)} %get-tuple-element.233), channel_id=1, source_target_pairs={{12,0},{13,1},{14,2},{15,3},{0,4},{1,5},{2,6},{3,7},{4,8},{5,9},{6... | collective-permute-start | bytes 294920 | tf_op jit(solution)/shard_map/while/body/eval_jaxpr/ppermute | solution.py:30
  35.2 5.4 %collective-permute-start.2 = (s32[384]{0:T(512)S(1)}, s32[384]{0:T(512)S(1)}, u32[]{:S(2)}, u32[]{:S(2)}) collective-permute-start(s32[384]{0:T(512)S(1)} %get-tuple-element.234), channel_id=1, source_target_pairs={{12,0},{13,1},{14,2},{15,3},{0,4},{1,5},{2,6},{3,7},{4,8},{5,9},{6... | collective-permute-start | bytes 4616 | tf_op jit(solution)/shard_map/while/body/eval_jaxpr/ppermute | solution.py:30
  35.5 6.5 %collective-permute-start = (bf16[384,1,128]{2,0,1:T(8,128)(2,1)S(1)}, bf16[384,1,128]{2,0,1:T(8,128)(2,1)S(1)}, u32[]{:S(2)}, u32[]{:S(2)}) collective-permute-start(bf16[384,1,128]{2,0,1:T(8,128)(2,1)S(1)} %get-tuple-element.232), channel_id=1, source_target_pairs={{12,0},{13,1},{14,2},{15,3},{0,4},{1,5},{2,6},{3,7},{4,8},{5,9},{6... | collective-permute-start | bytes 294920 | tf_op jit(solution)/shard_map/while/body/eval_jaxpr/ppermute | solution.py:30
  36.7 7.5 %collective-permute-start.1 = (bf16[384,1,128]{2,0,1:T(8,128)(2,1)S(1)}, bf16[384,1,128]{2,0,1:T(8,128)(2,1)S(1)}, u32[]{:S(2)}, u32[]{:S(2)}) collective-permute-start(bf16[384,1,128]{2,0,1:T(8,128)(2,1)S(1)} %get-tuple-element.233), channel_id=1, source_target_pairs={{12,0},{13,1},{14,2},{15,3},{0,4},{1,5},{2,6},{3,7},{4,8},{5,9},{6... | collective-permute-start | bytes 294920 | tf_op jit(solution)/shard_map/while/body/eval_jaxpr/ppermute | solution.py:30
  45.1 5.4 %collective-permute-start.2 = (s32[384]{0:T(512)S(1)}, s32[384]{0:T(512)S(1)}, u32[]{:S(2)}, u32[]{:S(2)}) collective-permute-start(s32[384]{0:T(512)S(1)} %get-tuple-element.234), channel_id=1, source_target_pairs={{12,0},{13,1},{14,2},{15,3},{0,4},{1,5},{2,6},{3,7},{4,8},{5,9},{6... | collective-permute-start | bytes 4616 | tf_op jit(solution)/shard_map/while/body/eval_jaxpr/ppermute | solution.py:30
  45.2 6.5 %collective-permute-start = (bf16[384,1,128]{2,0,1:T(8,128)(2,1)S(1)}, bf16[384,1,128]{2,0,1:T(8,128)(2,1)S(1)}, u32[]{:S(2)}, u32[]{:S(2)}) collective-permute-start(bf16[384,1,128]{2,0,1:T(8,128)(2,1)S(1)} %get-tuple-element.232), channel_id=1, source_target_pairs={{12,0},{13,1},{14,2},{15,3},{0,4},{1,5},{2,6},{3,7},{4,8},{5,9},{6... | collective-permute-start | bytes 294920 | tf_op jit(solution)/shard_map/while/body/eval_jaxpr/ppermute | solution.py:30
  46.2 6.7 %collective-permute-start.1 = (bf16[384,1,128]{2,0,1:T(8,128)(2,1)S(1)}, bf16[384,1,128]{2,0,1:T(8,128)(2,1)S(1)}, u32[]{:S(2)}, u32[]{:S(2)}) collective-permute-start(bf16[384,1,128]{2,0,1:T(8,128)(2,1)S(1)} %get-tuple-element.233), channel_id=1, source_target_pairs={{12,0},{13,1},{14,2},{15,3},{0,4},{1,5},{2,6},{3,7},{4,8},{5,9},{6... | collective-permute-start | bytes 294920 | tf_op jit(solution)/shard_map/while/body/eval_jaxpr/ppermute | solution.py:30
  54.1 1.5 %collective-permute-start.11 = (bf16[2,1,96,4,128]{4,2,3,0,1:T(8,128)(2,1)S(1)}, bf16[2,1,96,4,128]{4,2,3,0,1:T(8,128)(2,1)S(1)}, u32[]{:S(2)}, u32[]{:S(2)}) collective-permute-start(bf16[2,1,96,4,128]{4,2,3,0,1:T(8,128)(2,1)S(1)} %broadcast_select_fusion), channel_id=1, source_target_pairs={{0,1},{1,0},{2,3},{3,2},{4,5},{5,4},{6,7},{7,6},{8,9},{9,8},{10,11... | collective-permute-start | bytes 589832 | tf_op jit(solution)/shard_map/ppermute | solution.py:24
  55.8 7.0 %collective-permute-start.12 = (bf16[1,2,96,4,128]{4,2,3,1,0:T(8,128)(2,1)S(1)}, bf16[1,2,96,4,128]{4,2,3,1,0:T(8,128)(2,1)S(1)}, u32[]{:S(2)}, u32[]{:S(2)}) collective-permute-start(bf16[1,2,96,4,128]{4,2,3,1,0:T(8,128)(2,1)S(1)} %broadcast_select_fusion.2), channel_id=1, source_target_pairs={{0,2},{2,0},{1,3},{3,1},{4,6},{6,4},{5,7},{7,5},{8,10},{10,8},{9,1... | collective-permute-start | bytes 589832 | tf_op jit(solution)/shard_map/ppermute | solution.py:24
where the time goes:
time: 64 us; the launch traced here: 63.8 us
  waiting for transfers between devices  32.1 us (50%)
  starting transfers between devices  16.9 us (26%)
  other arithmetic  6.61 us (10%)
  matrix products  5.77 us (9%)
  local copies, waits for them, and re-layouts  1.75 us (3%)
    ppermute x10, waiting for transfers between devices, partner(): return lax.ppermute(block, axis, route)  19 us
    ppermute x9, waiting for transfers between devices, from_behind(): return lax.ppermute(block, axis, route)  13.1 us
    ppermute x9, starting transfers between devices, from_behind(): return lax.ppermute(block, axis, route)  9.26 us
    ppermute x10, starting transfers between devices, partner(): return lax.ppermute(block, axis, route)  7.64 us
    dot_general x4, matrix products, attend_block(): jnp.einsum('kgts,skd->kgtd', rounded, value_block, preferred_element_type...  3.62 us
    dot_general x4, matrix products, attend_block(): jnp.einsum('tkgd,skd->kgts', grouped, key_block, preferred_element_type=j...  2.16 us
    reduce_sum x4, other arithmetic, attend_block(): totals = totals * shrink + jnp.sum(weights, axis=-1)  2.08 us
  transfers between devices with their start and end apart: 19, of which 15 were waited for; matrix products, arithmetic and copies ran while one was open for 8% of the time, Pallas kernels for 0%

commit v1 on v0

v1 whole, which is shorter than its diff:
```python
import functools
import math

import jax
import jax.numpy as jnp
import numpy as np
from jax import lax
from jax.experimental import pallas as pl
from jax.experimental.pallas import tpu as pltpu
from jax.sharding import PartitionSpec as P

UNIT = 16
PIECES = 2
PLANE = 4


def rotary_tables(tokens, head_size, stride):
    half = head_size // 2
    inverse = 1000000.0 ** (-2.0 * np.arange(half) / head_size)
    angles = (stride * np.arange(tokens))[:, None] * inverse[None, :]
    wide = lambda x: np.concatenate([x, x], -1)
    return np.concatenate(
        [wide(np.cos(angles)), wide(np.sin(angles)), wide(np.tile(inverse, (8, 1)))]
    ).astype(np.float32)


def attend(
    n, kv_heads, per_group, tokens,
    place_ref, q_ref, k_ref, v_ref, table_ref, out_ref,
    gathered, q_rot, wide, small, m_ref, l_ref, acc_ref,
    recv_sem, send_sem,
):
    head_size = q_ref.shape[-1]
    heads = kv_heads * per_group
    rows = n // PLANE
    me = lax.axis_index("ctx")
    core = me % 2
    column = me // 2 % 2
    z = me // PLANE
    units = tokens // UNIT
    tile = 2 * UNIT
    tiles = tokens // tile
    per_piece = kv_heads // PIECES
    lanes = per_group * tile
    factor = math.log2(math.e) / math.sqrt(head_size)

    def device(row, col, cr):
        return row * PLANE + col * 2 + cr

    barrier = pltpu.get_barrier_semaphore()
    across = device(z, 1 - column, core)
    mate = device(z, column, 1 - core)
    below = me - PLANE
    above = me + PLANE

    def greet(target):
        pl.semaphore_signal(barrier, inc=1, device_id={"ctx": target})

    greet(across)
    greet(mate)

    @pl.when(z > 0)
    def _():
        greet(below)

    @pl.when(z < rows - 1)
    def _():
        greet(above)

    offset = place_ref[0].astype(jnp.float32)
    start = table_ref[2 * tokens : 2 * tokens + 8, :] * offset
    c0, s0 = jnp.cos(start)[:1], jnp.sin(start)[:1]
    ct, st = table_ref[:tokens, :], table_ref[tokens : 2 * tokens, :]
    lane = lax.broadcasted_iota(jnp.int32, (tokens, head_size), 1)
    cosine = ct * c0 - st * s0
    sine = st * c0 + ct * s0
    sine = jnp.where(lane < head_size // 2, -sine, sine)

    def rotated(x):
        return (x * cosine + pltpu.roll(x, head_size // 2, 1) * sine).astype(jnp.bfloat16)

    small[0] = k_ref[...].astype(jnp.float32)
    small[1] = v_ref[...].astype(jnp.float32)
    for h in range(kv_heads):
        p, at = h // per_piece, h % per_piece * 2 * units
        k = rotated(small[0, pl.ds(h, tokens, stride=kv_heads), :])
        gathered[p, at : at + units, me] = k.reshape(units, UNIT, head_size)
        v = small[1, pl.ds(h, tokens, stride=kv_heads), :].astype(jnp.bfloat16)
        gathered[p, at + units : at + 2 * units, me] = v.reshape(units, UNIT, head_size)
    own = jnp.full((UNIT, head_size), offset, jnp.float32)
    for p in range(PIECES):
        gathered[p, 2 * units * per_piece, me] = own.astype(jnp.bfloat16)

    def copy(slot, p, target, kind):
        return pltpu.make_async_remote_copy(
            src_ref=gathered.at[p, :, slot],
            dst_ref=gathered.at[p, :, slot],
            send_sem=send_sem.at[kind, slot, p],
            recv_sem=recv_sem.at[slot, p],
            device_id={"ctx": target},
        )

    def arrived(slot, p):
        copy(slot, p, mate, 0).wait_recv()

    def share(slot, p):
        copy(slot, p, across, 1).start()
        copy(slot, p, mate, 2).start()

    pl.semaphore_wait(barrier, 2 + (z > 0).astype(jnp.int32) + (z < rows - 1).astype(jnp.int32))

    for p in range(PIECES):

        @pl.when(z > 0)
        def _():
            copy(me, p, below, 0).start()

        @pl.when(z < rows - 1)
        def _():
            copy(me, p, above, 3).start()

        share(me, p)

    wide[...] = q_ref[...].astype(jnp.float32)
    for h in range(heads):
        k, g = divmod(h, per_group)
        q = rotated(wide[pl.ds(h, tokens, stride=heads), :])
        for t in range(tiles):
            q_rot[k, t * lanes + g * tile : t * lanes + (g + 1) * tile] = q[t * tile : (t + 1) * tile]

    width = tiles * lanes
    m_ref[...] = jnp.full(m_ref.shape, -jnp.inf, jnp.float32)
    l_ref[...] = jnp.zeros(l_ref.shape, jnp.float32)
    acc_ref[...] = jnp.zeros(acc_ref.shape, jnp.float32)

    keys_tile = PLANE * tile
    key_row = lax.broadcasted_iota(jnp.int32, (keys_tile, lanes), 0)
    key_at = key_row // (PLANE * UNIT) * UNIT + key_row % UNIT
    query_at = lax.broadcasted_iota(jnp.int32, (keys_tile, lanes), 1) % tile

    def attend_plane(row):
        first = row * PLANE

        def head(k, p, at):
            theirs = gathered[p, 2 * units * per_piece, pl.ds(first, PLANE)]
            theirs = theirs.astype(jnp.float32).reshape(PLANE * UNIT, head_size)
            theirs = jnp.concatenate([theirs] * (tile // UNIT), 0)
            reach = key_at + (theirs > offset).astype(jnp.int32)
            allowed = reach <= query_at
            scores = []
            for t in range(tiles):
                keys = gathered[p, pl.ds(at + 2 * t, 2), pl.ds(first, PLANE)]
                keys = keys.reshape(keys_tile, head_size)
                s = lax.dot_general(
                    keys, q_rot[k, t * lanes :],
                    (((1,), (1,)), ((), ())), preferred_element_type=jnp.float32,
                )
                diagonal = jnp.where(allowed, s[:, :lanes], -jnp.inf)
                scores.append([diagonal] + [s[:, i * lanes : (i + 1) * lanes] for i in range(1, tiles - t)])
            old = m_ref[k]
            weights = [[] for _ in range(tiles)]
            shrinks = []
            for i in range(tiles):
                span = slice(i * lanes, (i + 1) * lanes)
                mine = [scores[t][i - t] for t in range(i + 1)]
                top = old[:, span]
                for s in mine:
                    top = jnp.maximum(top, jnp.max(s, axis=0, keepdims=True))
                shrink = jnp.exp2((old[:, span] - top) * factor)
                total = l_ref[k, :, span] * shrink
                for t in range(i + 1):
                    w = jnp.exp2((mine[t] - top) * factor)
                    total += jnp.sum(w, axis=0, keepdims=True)
                    weights[t].append(w.astype(jnp.bfloat16))
                m_ref[k, :, span] = top
                l_ref[k, :, span] = total
                shrinks.append(shrink)
            sums = [acc_ref[k, :, i * lanes : (i + 1) * lanes] * shrinks[i] for i in range(tiles)]
            for t in range(tiles):
                values = gathered[p, pl.ds(at + units + 2 * t, 2), pl.ds(first, PLANE)]
                values = values.reshape(keys_tile, head_size)
                w = jnp.concatenate(weights[t], 1)
                o = lax.dot_general(
                    values, w, (((0,), (0,)), ((), ())), preferred_element_type=jnp.float32
                )
                for i in range(t, tiles):
                    sums[i] += o[:, (i - t) * lanes : (i - t + 1) * lanes]
            for i in range(tiles):
                acc_ref[k, :, i * lanes : (i + 1) * lanes] = sums[i]

        for p in range(PIECES):
            for col in range(2):
                arrived(device(row, col, 1 - core), p)

            @pl.loop(0, per_piece)
            def _(i):
                head(p * per_piece + i, p, i * 2 * units)

    def either(step, do):
        @pl.when(z >= step)
        def _():
            do(z - step, False)

        @pl.when(z + step < rows)
        def _():
            do(z + step, True)

    def relay_column(step):
        for p in range(PIECES):

            def do(row, from_above):
                slot = device(row, column, core)
                arrived(slot, p)
                if from_above:

                    @pl.when(z > 0)
                    def _():
                        copy(slot, p, below, 0).start()
                else:

                    @pl.when(z < rows - 1)
                    def _():
                        copy(slot, p, above, 3).start()
                share(slot, p)

            either(step, do)

    def relay_across(row):
        for p in range(PIECES):
            slot = device(row, 1 - column, core)
            arrived(slot, p)
            copy(slot, p, mate, 2).start()

    def finish(row, from_above):
        relay_across(row)
        attend_plane(row)

    relay_column(1)
    relay_across(z)
    attend_plane(z)

    @pl.loop(1, rows)
    def _(step):
        @pl.when(step + 1 < rows)
        def _():
            relay_column(step + 1)

        either(step, finish)

    for k in range(kv_heads):
        o = (acc_ref[k] / l_ref[k]).T
        for t in range(tiles):
            for g in range(per_group):
                at = t * lanes + g * tile
                wide[pl.ds(t * tile * heads + k * per_group + g, tile, stride=heads), :] = o[at : at + tile]
    out_ref[...] = wide[...].astype(jnp.bfloat16)

    def sent(row, from_above):
        for p in range(PIECES):
            slot = device(row, column, core)
            if from_above:

                @pl.when(z > 0)
                def _():
                    copy(slot, p, below, 0).wait_send()
            else:

                @pl.when(z < rows - 1)
                def _():
                    copy(slot, p, above, 3).wait_send()
            copy(slot, p, across, 1).wait_send()
            copy(slot, p, mate, 2).wait_send()
            copy(device(row, 1 - column, core), p, mate, 2).wait_send()

    @pl.loop(1, rows)
    def _(step):
        either(step, sent)

    sent(z, False)
    for p in range(PIECES):

        @pl.when(z > 0)
        def _():
            copy(me, p, below, 0).wait_send()


def solution(mesh):
    n = mesh.shape["ctx"]

    def shards(queries, keys, values, positions):
        tokens, heads, head_size = queries.shape
        kv_heads = keys.shape[1]
        per_group = heads // kv_heads
        table = rotary_tables(tokens, head_size, n)
        tile = 2 * UNIT
        width = tokens * per_group
        blocks = 2 * (tokens // UNIT) * (kv_heads // PIECES) + 1
        vmem = pl.BlockSpec(memory_space=pltpu.VMEM)
        out = pl.pallas_call(
            functools.partial(attend, n, kv_heads, per_group, tokens),
            out_shape=jax.ShapeDtypeStruct((tokens * heads, head_size), jnp.bfloat16),
            in_specs=[pl.BlockSpec(memory_space=pltpu.SMEM)] + [vmem] * 4,
            out_specs=vmem,
            scratch_shapes=[
                pltpu.VMEM((PIECES, blocks, n, UNIT, head_size), jnp.bfloat16),
                pltpu.VMEM((kv_heads, width, head_size), jnp.bfloat16),
                pltpu.VMEM((tokens * heads, head_size), jnp.float32),
                pltpu.VMEM((2, tokens * kv_heads, head_size), jnp.float32),
                pltpu.VMEM((kv_heads, 1, width), jnp.float32),
                pltpu.VMEM((kv_heads, 1, width), jnp.float32),
                pltpu.VMEM((kv_heads, head_size, width), jnp.float32),
                pltpu.SemaphoreType.DMA((n, PIECES)),
                pltpu.SemaphoreType.DMA((4, n, PIECES)),
            ],
            compiler_params=pltpu.CompilerParams(
                collective_id=0, has_side_effects=True, vmem_limit_bytes=48 * 1024 * 1024
            ),
        )(
            positions,
            queries.reshape(tokens * heads, head_size),
            keys.reshape(tokens * kv_heads, head_size),
            values.reshape(tokens * kv_heads, head_size),
            table,
        )
        return out.reshape(tokens, heads, head_size)

    placed = (
        P(("groups", "ctx"), None, None),
        P(("groups", "ctx"), None, None),
        P(("groups", "ctx"), None, None),
        P(("groups", "ctx")),
    )
    return jax.shard_map(
        shards,
        mesh=mesh,
        in_specs=placed,
        out_specs=P(("groups", "ctx"), None, None),
        check_vma=False,
    )
```

time: 64 us -> 34.6 us (0.54)
  waiting for transfers between devices: 32.1 us -> 0 us
  Pallas kernels: 0 us -> 29.3 us
  starting transfers between devices: 16.9 us -> 0 us
  other arithmetic: 6.61 us -> 0 us
  matrix products: 5.77 us -> 0 us
  local copies, waits for them, and re-layouts: 1.75 us -> 5.08 us
    ppermute x19 -> x0, waiting for transfers between devices: 32.1 us -> none  [the longest x10 19 us: partner(): return lax.ppermute(block, axis, route)]
    pallas_call x0 -> x1, Pallas kernels: none -> 29.3 us  [shards(): pl.pallas_call(functools.partial(attend, n, kv_heads, per_group, tokens),...]
    ppermute x19 -> x0, starting transfers between devices: 16.9 us -> none  [the longest x9 9.26 us: from_behind(): return lax.ppermute(block, axis, route)]
    dot_general x8 -> x0, matrix products: 5.77 us -> none  [the longest x4 3.62 us: attend_block(): jnp.einsum('kgts,skd->kgtd', rounded, value_block, preferred_element_type...]
    unnamed x8 -> x11, local copies, waits for them, and re-layouts: 0.02 us -> 5.08 us
    reduce_sum x4 -> x0, other arithmetic: 2.08 us -> none  [attend_block(): totals = totals * shrink + jnp.sum(weights, axis=-1)]
    convert_element_type x4 -> x0, other arithmetic: 2.01 us -> none  [the longest x2 1.07 us: rotate(): floats = tensor.astype(jnp.float32)]
    another operation x22 -> x0, other arithmetic: 1.06 us -> none
  transfers between devices with their start and end apart: 19 -> 0, of which waited for: 15 -> 0; matrix products, arithmetic and copies ran while one was open for 8% -> 0% of each run, Pallas kernels for 0% -> 0%
where the time goes in v1:
time: 34.6 us; the launch traced here: 34.4 us
  Pallas kernels  29.3 us (85%)
  local copies, waits for them, and re-layouts  5.08 us (15%)
    pallas_call x1, Pallas kernels, shards(): pl.pallas_call(functools.partial(attend, n, kv_heads, per_group, tokens),...  29.3 us
    unnamed x11, local copies, waits for them, and re-layouts  5.08 us

profile of v1, /device:TPU:0, one launch (start us, length us, event | category | flops | bytes accessed | tf_op | source)
XLA Modules:
  0.0 34.4 jit_solution(882166278062007751)
XLA Ops:
  0.0 0.0 copy-start.4
  0.0 0.7 %copy-done.4 = s32[96]{0:T(128)S(1)} copy-done((s32[96]{0:T(128)S(1)}, s32[96]{0:T(128)}, u32[]{:S(2)}) %copy-start.4) | copy-done | bytes 408
  0.7 0.0 copy-start
  0.7 1.0 %copy-done = bf16[96,16,128]{2,1,0:T(8,128)(2,1)S(1)} copy-done((bf16[96,16,128]{2,1,0:T(8,128)(2,1)S(1)}, bf16[96,16,128]{2,1,0:T(8,128)(2,1)}, u32[]{:S(2)}) %copy-start) | copy-done | bytes 393240
  1.7 0.0 copy-start.1
  1.7 0.9 %copy-done.1 = f32[200,128]{1,0:T(8,128)S(1)} copy-done((f32[200,128]{1,0:T(8,128)S(1)}, f32[200,128]{1,0:T(8,128)}, u32[]{:S(2)}) %copy-start.1) | copy-done | bytes 102424
  2.5 0.0 copy-start.2
  2.5 0.9 %copy-done.2 = bf16[96,4,128]{2,1,0:T(4,128)(2,1)S(1)} copy-done((bf16[96,4,128]{2,1,0:T(4,128)(2,1)S(1)}, bf16[96,4,128]{2,1,0:T(4,128)(2,1)}, u32[]{:S(2)}) %copy-start.2) | copy-done | bytes 98328
  3.4 0.0 copy-start.3
  3.4 0.9 %copy-done.3 = bf16[96,4,128]{2,1,0:T(4,128)(2,1)S(1)} copy-done((bf16[96,4,128]{2,1,0:T(4,128)(2,1)S(1)}, bf16[96,4,128]{2,1,0:T(4,128)(2,1)}, u32[]{:S(2)}) %copy-start.3) | copy-done | bytes 98328
  4.3 29.3 %shard_map.55 = bf16[1536,128]{1,0:T(8,128)(2,1)S(1)} custom-call(s32[96]{0:T(128)S(1)} %copy-done.4, bf16[1536,128]{1,0:T(8,128)(2,1)S(1)} %bitcast.5, bf16[384,128]{1,0:T(8,128)(2,1)S(1)} %bitcast.6, bf16[384,128]{1,0:T(8,128)(2,1)S(1)} %bitcast.7, f32[200,128]{1,0:T(8,128)S(1)} %copy-done.1), custom_call_target="tpu_custom_call" | custom-call | tf_op jit(solution)/shard_map/pallas_call | solution.py:299
  33.6 0.7 %copy.7 = bf16[96,16,128]{2,1,0:T(8,128)(2,1)} copy(bf16[96,16,128]{2,1,0:T(8,128)(2,1)S(1)} %bitcast.4) | data formatting | bytes 786432
Async XLA Ops:
  0.0 0.7 %copy-start.4 = (s32[96]{0:T(128)S(1)}, s32[96]{0:T(128)}, u32[]{:S(2)}) copy-start(s32[96]{0:T(128)} %place_ref.1) | copy-start | bytes 1156
  0.7 1.0 %copy-start = (bf16[96,16,128]{2,1,0:T(8,128)(2,1)S(1)}, bf16[96,16,128]{2,1,0:T(8,128)(2,1)}, u32[]{:S(2)}) copy-start(bf16[96,16,128]{2,1,0:T(8,128)(2,1)} %param.5) | copy-start | bytes 1179652
  1.7 0.9 %copy-start.1 = (f32[200,128]{1,0:T(8,128)S(1)}, f32[200,128]{1,0:T(8,128)}, u32[]{:S(2)}) copy-start(f32[200,128]{1,0:T(8,128)} %constant.2.clone.table_ref) | copy-start | bytes 307204
  2.5 0.9 %copy-start.2 = (bf16[96,4,128]{2,1,0:T(4,128)(2,1)S(1)}, bf16[96,4,128]{2,1,0:T(4,128)(2,1)}, u32[]{:S(2)}) copy-start(bf16[96,4,128]{2,1,0:T(4,128)(2,1)} %param.6) | copy-start | bytes 294916
  3.4 0.9 %copy-start.3 = (bf16[96,4,128]{2,1,0:T(4,128)(2,1)S(1)}, bf16[96,4,128]{2,1,0:T(4,128)(2,1)}, u32[]{:S(2)}) copy-start(bf16[96,4,128]{2,1,0:T(4,128)(2,1)} %param.7) | copy-start | bytes 294916

commit v2 on v1

--- a/solution.py
+++ b/solution.py
@@ -10,7 +10,7 @@
 from jax.sharding import PartitionSpec as P
 
 UNIT = 16
-PIECES = 2
+PIECES = 4
 PLANE = 4
 
 
@@ -26,10 +26,19 @@
 
 def attend(
     n, kv_heads, per_group, tokens,
-    place_ref, q_ref, k_ref, v_ref, table_ref, out_ref,
+    place_hbm, q_hbm, k_hbm, v_hbm, table_hbm, out_ref,
     gathered, q_rot, wide, small, m_ref, l_ref, acc_ref,
-    recv_sem, send_sem,
+    place_ref, q_ref, k_ref, v_ref, table_ref,
+    recv_sem, send_sem, load_sem,
 ):
+    loads = [
+        pltpu.make_async_copy(src, dst, load_sem.at[i])
+        for i, (src, dst) in enumerate(
+            [(place_hbm, place_ref), (table_hbm, table_ref), (k_hbm, k_ref), (v_hbm, v_ref), (q_hbm, q_ref)]
+        )
+    ]
+    for load in loads:
+        load.start()
     head_size = q_ref.shape[-1]
     heads = kv_heads * per_group
     rows = n // PLANE
@@ -67,6 +76,8 @@
     def _():
         greet(above)
 
+    for load in loads[:2]:
+        load.wait()
     offset = place_ref[0].astype(jnp.float32)
     start = table_ref[2 * tokens : 2 * tokens + 8, :] * offset
     c0, s0 = jnp.cos(start)[:1], jnp.sin(start)[:1]
@@ -79,22 +90,26 @@
     def rotated(x):
         return (x * cosine + pltpu.roll(x, head_size // 2, 1) * sine).astype(jnp.bfloat16)
 
+    for load in loads[2:4]:
+        load.wait()
     small[0] = k_ref[...].astype(jnp.float32)
     small[1] = v_ref[...].astype(jnp.float32)
     for h in range(kv_heads):
-        p, at = h // per_piece, h % per_piece * 2 * units
+        at = 1 + h * 2 * units
         k = rotated(small[0, pl.ds(h, tokens, stride=kv_heads), :])
-        gathered[p, at : at + units, me] = k.reshape(units, UNIT, head_size)
+        gathered[me, at : at + units] = k.reshape(units, UNIT, head_size)
         v = small[1, pl.ds(h, tokens, stride=kv_heads), :].astype(jnp.bfloat16)
-        gathered[p, at + units : at + 2 * units, me] = v.reshape(units, UNIT, head_size)
+        gathered[me, at + units : at + 2 * units] = v.reshape(units, UNIT, head_size)
     own = jnp.full((UNIT, head_size), offset, jnp.float32)
-    for p in range(PIECES):
-        gathered[p, 2 * units * per_piece, me] = own.astype(jnp.bfloat16)
+    gathered[me, 0] = own.astype(jnp.bfloat16)
 
     def copy(slot, p, target, kind):
+        blocks = 2 * units * per_piece
+        first = 1 + p * blocks if p else 0
+        part = gathered.at[slot, pl.ds(first, 1 + (p + 1) * blocks - first)]
         return pltpu.make_async_remote_copy(
-            src_ref=gathered.at[p, :, slot],
-            dst_ref=gathered.at[p, :, slot],
+            src_ref=part,
+            dst_ref=part,
             send_sem=send_sem.at[kind, slot, p],
             recv_sem=recv_sem.at[slot, p],
             device_id={"ctx": target},
@@ -121,6 +136,7 @@
 
         share(me, p)
 
+    loads[4].wait()
     wide[...] = q_ref[...].astype(jnp.float32)
     for h in range(heads):
         k, g = divmod(h, per_group)
@@ -135,21 +151,22 @@
 
     keys_tile = PLANE * tile
     key_row = lax.broadcasted_iota(jnp.int32, (keys_tile, lanes), 0)
-    key_at = key_row // (PLANE * UNIT) * UNIT + key_row % UNIT
+    key_at = key_row % tile
     query_at = lax.broadcasted_iota(jnp.int32, (keys_tile, lanes), 1) % tile
 
     def attend_plane(row):
         first = row * PLANE
 
-        def head(k, p, at):
-            theirs = gathered[p, 2 * units * per_piece, pl.ds(first, PLANE)]
-            theirs = theirs.astype(jnp.float32).reshape(PLANE * UNIT, head_size)
-            theirs = jnp.concatenate([theirs] * (tile // UNIT), 0)
+        def head(k):
+            at = 1 + k * 2 * units
+            theirs = gathered[pl.ds(first, PLANE), 0].astype(jnp.float32)
+            theirs = jnp.concatenate([theirs[:, None]] * (tile // UNIT), 1)
+            theirs = theirs.reshape(keys_tile, head_size)
             reach = key_at + (theirs > offset).astype(jnp.int32)
             allowed = reach <= query_at
             scores = []
             for t in range(tiles):
-                keys = gathered[p, pl.ds(at + 2 * t, 2), pl.ds(first, PLANE)]
+                keys = gathered[pl.ds(first, PLANE), pl.ds(at + 2 * t, 2)]
                 keys = keys.reshape(keys_tile, head_size)
                 s = lax.dot_general(
                     keys, q_rot[k, t * lanes :],
@@ -177,7 +194,7 @@
                 shrinks.append(shrink)
             sums = [acc_ref[k, :, i * lanes : (i + 1) * lanes] * shrinks[i] for i in range(tiles)]
             for t in range(tiles):
-                values = gathered[p, pl.ds(at + units + 2 * t, 2), pl.ds(first, PLANE)]
+                values = gathered[pl.ds(first, PLANE), pl.ds(at + units + 2 * t, 2)]
                 values = values.reshape(keys_tile, head_size)
                 w = jnp.concatenate(weights[t], 1)
                 o = lax.dot_general(
@@ -194,7 +211,7 @@
 
             @pl.loop(0, per_piece)
             def _(i):
-                head(p * per_piece + i, p, i * 2 * units)
+                head(p * per_piece + i)
 
     def either(step, do):
         @pl.when(z >= step)
@@ -294,26 +311,33 @@
         table = rotary_tables(tokens, head_size, n)
         tile = 2 * UNIT
         width = tokens * per_group
-        blocks = 2 * (tokens // UNIT) * (kv_heads // PIECES) + 1
+        blocks = 1 + 2 * (tokens // UNIT) * kv_heads
         vmem = pl.BlockSpec(memory_space=pltpu.VMEM)
+        hbm = pl.BlockSpec(memory_space=pl.ANY)
         out = pl.pallas_call(
             functools.partial(attend, n, kv_heads, per_group, tokens),
             out_shape=jax.ShapeDtypeStruct((tokens * heads, head_size), jnp.bfloat16),
-            in_specs=[pl.BlockSpec(memory_space=pltpu.SMEM)] + [vmem] * 4,
+            in_specs=[hbm] * 5,
             out_specs=vmem,
             scratch_shapes=[
-                pltpu.VMEM((PIECES, blocks, n, UNIT, head_size), jnp.bfloat16),
+                pltpu.VMEM((n, blocks, UNIT, head_size), jnp.bfloat16),
                 pltpu.VMEM((kv_heads, width, head_size), jnp.bfloat16),
                 pltpu.VMEM((tokens * heads, head_size), jnp.float32),
                 pltpu.VMEM((2, tokens * kv_heads, head_size), jnp.float32),
                 pltpu.VMEM((kv_heads, 1, width), jnp.float32),
                 pltpu.VMEM((kv_heads, 1, width), jnp.float32),
                 pltpu.VMEM((kv_heads, head_size, width), jnp.float32),
+                pltpu.SMEM((tokens,), jnp.int32),
+                pltpu.VMEM((tokens * heads, head_size), jnp.bfloat16),
+                pltpu.VMEM((tokens * kv_heads, head_size), jnp.bfloat16),
+                pltpu.VMEM((tokens * kv_heads, head_size), jnp.bfloat16),
+                pltpu.VMEM(table.shape, jnp.float32),
                 pltpu.SemaphoreType.DMA((n, PIECES)),
                 pltpu.SemaphoreType.DMA((4, n, PIECES)),
+                pltpu.SemaphoreType.DMA((5,)),
             ],
             compiler_params=pltpu.CompilerParams(
-                collective_id=0, has_side_effects=True, vmem_limit_bytes=48 * 1024 * 1024
+                collective_id=0, has_side_effects=True, vmem_limit_bytes=67043328
             ),
         )(
             positions,

time: 34.6 us -> 32.2 us (0.931)
  local copies, waits for them, and re-layouts: 5.08 us -> 1.77 us
  Pallas kernels: 29.3 us -> 30.3 us
    unnamed x11 -> x1, local copies, waits for them, and re-layouts: 5.08 us -> 1.77 us
    pallas_call x1, Pallas kernels: 29.3 us -> 30.3 us  [shards(): pl.pallas_call(functools.partial(attend, n, kv_heads, per_group, tokens),...]
where the time goes in v2:
time: 32.2 us; the launch traced here: 32.1 us
  Pallas kernels  30.3 us (94%)
  local copies, waits for them, and re-layouts  1.77 us (5%)
    pallas_call x1, Pallas kernels, shards(): pl.pallas_call(functools.partial(attend, n, kv_heads, per_group, tokens),...  30.3 us
    unnamed x1, local copies, waits for them, and re-layouts  1.77 us

profile of v2, /device:TPU:0, one launch (start us, length us, event | category | flops | bytes accessed | tf_op | source)
XLA Modules:
  0.0 32.1 jit_solution(11745166724074982335)
XLA Ops:
  0.0 30.3 %shard_map.55 = bf16[1536,128]{1,0:T(8,128)(2,1)} custom-call(s32[96]{0:T(128)} %place_hbm.1, bf16[1536,128]{1,0:T(8,128)(2,1)} %bitcast.5, bf16[384,128]{1,0:T(8,128)(2,1)} %bitcast.6, bf16[384,128]{1,0:T(8,128)(2,1)} %bitcast.7, f32[200,128]{1,0:T(8,128)} %constant.2.clone.table_hbm), custom_call_target="tpu_custom_call" | custom-call | tf_op jit(solution)/shard_map/pallas_call | solution.py:317
  30.3 1.8 %copy.7 = bf16[96,16,128]{2,1,0:T(8,128)(2,1)} copy(bf16[96,16,128]{2,1,0:T(8,128)(2,1)} %bitcast.4) | data formatting | bytes 786432

commit v3 on v2

--- a/solution.py
+++ b/solution.py
@@ -10,7 +10,7 @@
 from jax.sharding import PartitionSpec as P
 
 UNIT = 16
-PIECES = 4
+PIECES = 2
 PLANE = 4
 
 
@@ -209,8 +209,7 @@
             for col in range(2):
                 arrived(device(row, col, 1 - core), p)
 
-            @pl.loop(0, per_piece)
-            def _(i):
+            for i in range(per_piece):
                 head(p * per_piece + i)
 
     def either(step, do):
@@ -337,14 +336,19 @@
                 pltpu.SemaphoreType.DMA((5,)),
             ],
             compiler_params=pltpu.CompilerParams(
-                collective_id=0, has_side_effects=True, vmem_limit_bytes=67043328
+                collective_id=0, has_side_effects=True, vmem_limit_bytes=48*1024*1024
             ),
         )(
-            positions,
-            queries.reshape(tokens * heads, head_size),
-            keys.reshape(tokens * kv_heads, head_size),
-            values.reshape(tokens * kv_heads, head_size),
-            table,
+            *(
+                pltpu.with_memory_space_constraint(x, pltpu.HBM)
+                for x in (
+                    positions,
+                    queries.reshape(tokens * heads, head_size),
+                    keys.reshape(tokens * kv_heads, head_size),
+                    values.reshape(tokens * kv_heads, head_size),
+                    jnp.asarray(table),
+                )
+            )
         )
         return out.reshape(tokens, heads, head_size)
 

time: 32.2 us -> 29.1 us (0.904)
  Pallas kernels: 30.3 us -> 28.2 us
  local copies, waits for them, and re-layouts: 1.77 us -> 0.75 us
    pallas_call x1, Pallas kernels: 30.3 us -> 28.2 us  [shards(): pl.pallas_call(functools.partial(attend, n, kv_heads, per_group, tokens),...]
    unnamed x1, local copies, waits for them, and re-layouts: 1.77 us -> 0.75 us
where the time goes in v3:
time: 29.1 us; the launch traced here: 29 us
  Pallas kernels  28.2 us (97%)
  local copies, waits for them, and re-layouts  0.75 us (3%)
    pallas_call x1, Pallas kernels, shards(): pl.pallas_call(functools.partial(attend, n, kv_heads, per_group, tokens),...  28.2 us
    unnamed x1, local copies, waits for them, and re-layouts  0.75 us

profile of v3, /device:TPU:0, one launch (start us, length us, event | category | flops | bytes accessed | tf_op | source)
XLA Modules:
  0.0 29.0 jit_solution(1929838172945037464)
XLA Ops:
  0.0 28.2 %shard_map.55 = bf16[1536,128]{1,0:T(8,128)(2,1)S(1)} custom-call(s32[96]{0:T(128)} %place_hbm.1, bf16[1536,128]{1,0:T(8,128)(2,1)} %bitcast.5, bf16[384,128]{1,0:T(8,128)(2,1)} %bitcast.6, bf16[384,128]{1,0:T(8,128)(2,1)} %bitcast.7, f32[200,128]{1,0:T(8,128)} %constant.2.clone.table_hbm), custom_call_target="tpu_custom_call" | custom-call | tf_op jit(solution)/shard_map/pallas_call | solution.py:316
  28.2 0.7 %copy.7 = bf16[96,16,128]{2,1,0:T(8,128)(2,1)} copy(bf16[96,16,128]{2,1,0:T(8,128)(2,1)S(1)} %bitcast.4) | data formatting | bytes 786432

commit v4 on v3

--- a/solution.py
+++ b/solution.py
@@ -37,7 +37,7 @@
             [(place_hbm, place_ref), (table_hbm, table_ref), (k_hbm, k_ref), (v_hbm, v_ref), (q_hbm, q_ref)]
         )
     ]
-    for load in loads:
+    for load in loads[:4]:
         load.start()
     head_size = q_ref.shape[-1]
     heads = kv_heads * per_group
@@ -92,6 +92,7 @@
 
     for load in loads[2:4]:
         load.wait()
+    loads[4].start()
     small[0] = k_ref[...].astype(jnp.float32)
     small[1] = v_ref[...].astype(jnp.float32)
     for h in range(kv_heads):
@@ -247,10 +248,6 @@
             arrived(slot, p)
             copy(slot, p, mate, 2).start()
 
-    def finish(row, from_above):
-        relay_across(row)
-        attend_plane(row)
-
     relay_column(1)
     relay_across(z)
     attend_plane(z)
@@ -261,7 +258,8 @@
         def _():
             relay_column(step + 1)
 
-        either(step, finish)
+        either(step, lambda row, from_above: relay_across(row))
+        either(step, lambda row, from_above: attend_plane(row))
 
     for k in range(kv_heads):
         o = (acc_ref[k] / l_ref[k]).T

time: 29.1 us -> 29.1 us (level)
  no operation moved by 1% of the time
where the time goes in v4:
time: 29.1 us; the launch traced here: 29 us
  Pallas kernels  28.2 us (97%)
  local copies, waits for them, and re-layouts  0.75 us (3%)
    pallas_call x1, Pallas kernels, shards(): pl.pallas_call(functools.partial(attend, n, kv_heads, per_group, tokens),...  28.2 us
    unnamed x1, local copies, waits for them, and re-layouts  0.75 us

profile of v4, /device:TPU:0, one launch (start us, length us, event | category | flops | bytes accessed | tf_op | source)
XLA Modules:
  0.0 29.0 jit_solution(11272438724829362787)
XLA Ops:
  0.0 28.2 %shard_map.55 = bf16[1536,128]{1,0:T(8,128)(2,1)S(1)} custom-call(s32[96]{0:T(128)} %place_hbm.1, bf16[1536,128]{1,0:T(8,128)(2,1)} %bitcast.5, bf16[384,128]{1,0:T(8,128)(2,1)} %bitcast.6, bf16[384,128]{1,0:T(8,128)(2,1)} %bitcast.7, f32[200,128]{1,0:T(8,128)} %constant.2.clone.table_hbm), custom_call_target="tpu_custom_call" | custom-call | tf_op jit(solution)/shard_map/pallas_call | solution.py:314
  28.2 0.7 %copy.7 = bf16[96,16,128]{2,1,0:T(8,128)(2,1)} copy(bf16[96,16,128]{2,1,0:T(8,128)(2,1)S(1)} %bitcast.4) | data formatting | bytes 786432

commit v5 on v4

--- a/solution.py
+++ b/solution.py
@@ -37,8 +37,6 @@
             [(place_hbm, place_ref), (table_hbm, table_ref), (k_hbm, k_ref), (v_hbm, v_ref), (q_hbm, q_ref)]
         )
     ]
-    for load in loads[:4]:
-        load.start()
     head_size = q_ref.shape[-1]
     heads = kv_heads * per_group
     rows = n // PLANE
@@ -76,6 +74,9 @@
     def _():
         greet(above)
 
+    for load in loads[:4]:
+        load.start()
+
     for load in loads[:2]:
         load.wait()
     offset = place_ref[0].astype(jnp.float32)
@@ -126,6 +127,7 @@
     pl.semaphore_wait(barrier, 2 + (z > 0).astype(jnp.int32) + (z < rows - 1).astype(jnp.int32))
 
     for p in range(PIECES):
+        share(me, p)
 
         @pl.when(z > 0)
         def _():
@@ -135,7 +137,6 @@
         def _():
             copy(me, p, above, 3).start()
 
-        share(me, p)
 
     loads[4].wait()
     wide[...] = q_ref[...].astype(jnp.float32)

time: 29.1 us -> 29.1 us (level)
  no operation moved by 1% of the time
where the time goes in v5:
time: 29.1 us; the launch traced here: 29 us
  Pallas kernels  28.2 us (97%)
  local copies, waits for them, and re-layouts  0.75 us (3%)
    pallas_call x1, Pallas kernels, shards(): pl.pallas_call(functools.partial(attend, n, kv_heads, per_group, tokens),...  28.2 us
    unnamed x1, local copies, waits for them, and re-layouts  0.75 us

profile of v5, /device:TPU:0, one launch (start us, length us, event | category | flops | bytes accessed | tf_op | source)
XLA Modules:
  0.0 29.0 jit_solution(14490868285939477899)
XLA Ops:
  0.0 28.2 %shard_map.55 = bf16[1536,128]{1,0:T(8,128)(2,1)S(1)} custom-call(s32[96]{0:T(128)} %place_hbm.1, bf16[1536,128]{1,0:T(8,128)(2,1)} %bitcast.5, bf16[384,128]{1,0:T(8,128)(2,1)} %bitcast.6, bf16[384,128]{1,0:T(8,128)(2,1)} %bitcast.7, f32[200,128]{1,0:T(8,128)} %constant.2.clone.table_hbm), custom_call_target="tpu_custom_call" | custom-call | tf_op jit(solution)/shard_map/pallas_call | solution.py:315
  28.2 0.7 %copy.7 = bf16[96,16,128]{2,1,0:T(8,128)(2,1)} copy(bf16[96,16,128]{2,1,0:T(8,128)(2,1)S(1)} %bitcast.4) | data formatting | bytes 786432
